TPU v7x, 32 devices: a whole 2x2x4 slice. The times are simulated.
32 devices in a mesh: ep: 8 (over z, y), tp: 4 (over x, core).
Axes of the slice: x: 2, y: 2, z: 4, core: 2. Of those that a mesh axis runs over, the one named last changes fastest.
Arguments:
- tokens: bfloat16 [4096, 2048], P(('ep', 'tp')), may hold values from -6 to 6
- norm_gain: float32 [2048], replicated, may hold values from 0.1 to 1.9
- expert_ids: int32 [4096, 6], P(('ep', 'tp')), may hold values from 0 to 15, as said below
- slot_index: int32 [4096, 6], P(('ep', 'tp')), may hold values from 0 to 63, as said below
- dropped: int32 [4096, 6], P(('ep', 'tp')), may hold values from 0 to 1, as said below
- gates: float32 [4096, 6], P(('ep', 'tp')), may hold values from 0.05 to 0.8
- w_gate: bfloat16 [16, 2048, 704], P('ep', None, 'tp'), may hold values from -0.125 to 0.125
- w_up: bfloat16 [16, 2048, 704], P('ep', None, 'tp'), may hold values from -0.125 to 0.125
- w_down: bfloat16 [16, 2048, 704], P('ep', None, 'tp'), may hold values from -0.21875 to 0.21875
- shared_gate: bfloat16 [2048, 1408], P(None, 'tp'), may hold values from -0.125 to 0.125
- shared_up: bfloat16 [2048, 1408], P(None, 'tp'), may hold values from -0.125 to 0.125
- shared_down: bfloat16 [1408, 2048], replicated, may hold values from -0.15625 to 0.15625
Outputs:
- layer_out: bfloat16 [4096, 2048], P(('ep', 'tp'))
Inputs may be any that keep to these rules, and one draw needn't show every extreme that they name: `expert_ids`: each token names 6 different experts; some expert has 64 kept pairs from the tokens of every device. `slot_index`: for a kept pair, its place among the slots of its expert for the tokens of its device (the tokens n with one value of n // 128); the kept pairs of one device and one expert have distinct places; 0 for a dropped pair. `dropped`: 1 for the pairs of a device and an expert beyond the 64 that are kept.
All inputs are finite; a program needn't handle non-finite values.
Results may differ from a plain program's by a relative error of at most 0.0054.
Values may be sent and summed in bfloat16 or wider, within the bound.
A program may use at most 128 MiB of HBM per device.

v0:
```python
import jax
import jax.numpy as jnp
from jax import lax
from jax.sharding import PartitionSpec as P

TOP = 6
EXP_DEV = 2
TOK_DEV = 128
norm_eps = 1e-06


def swiglu(left, right):
    return jax.nn.silu(left) * right


def on_device(
    tokens,
    norm_gain,
    expert_ids,
    slot_index,
    dropped,
    gates,
    w_gate,
    w_up,
    w_down,
    shared_gate,
    shared_up,
    shared_down,
):
    n_expert_groups = lax.axis_size("ep")
    experts = EXP_DEV * n_expert_groups
    capacity = TOK_DEV * TOP * 4 // (experts * 3)
    model_width = tokens.shape[1]
    local_rows = tokens.shape[0]
    values = tokens.astype(jnp.float32)
    scale = lax.rsqrt(jnp.mean(values * values, axis=-1, keepdims=True) + norm_eps)
    normed = (values * scale * norm_gain).astype(jnp.bfloat16)
    destination_position = expert_ids * capacity + slot_index
    kept_pair = dropped == 0
    matrix_breadth = lax.iota(jnp.int32, experts * capacity)
    matches = (destination_position[:, :, None] == matrix_breadth[None, None, :]) & kept_pair[
        :, :, None
    ]
    dispatch_table = jnp.any(matches, axis=1).astype(jnp.bfloat16)
    outgoing = lax.dot_general(
        dispatch_table, normed, (((0,), (0,)), ((), ())), preferred_element_type=jnp.float32
    ).astype(jnp.bfloat16)
    boxes = outgoing.reshape(n_expert_groups, EXP_DEV, capacity, model_width)
    received = lax.all_to_all(boxes, "ep", split_axis=0, concat_axis=0, tiled=True)
    gate_all = lax.all_gather(w_gate, "tp", axis=2, tiled=True)
    up_all = lax.all_gather(w_up, "tp", axis=2, tiled=True)
    down_all = lax.all_gather(w_down, "tp", axis=2, tiled=True)
    gate_act = jnp.einsum("iecd,edf->iecf", received, gate_all, preferred_element_type=jnp.float32)
    up_act = jnp.einsum("iecd,edf->iecf", received, up_all, preferred_element_type=jnp.float32)
    hidden = swiglu(gate_act, up_act).astype(jnp.bfloat16)
    expert_out = jnp.einsum(
        "iecf,edf->iecd", hidden, down_all, preferred_element_type=jnp.float32
    ).astype(jnp.bfloat16)
    returned_output = lax.all_to_all(expert_out, "ep", split_axis=0, concat_axis=0, tiled=True)
    returned_rows = returned_output.reshape(experts * capacity, model_width)
    shard_piece = lax.all_gather(normed, "tp", axis=0, tiled=True)
    gate_act = jnp.dot(shard_piece, shared_gate, preferred_element_type=jnp.float32)
    up_act = jnp.dot(shard_piece, shared_up, preferred_element_type=jnp.float32)
    partial_hidden = swiglu(gate_act, up_act).astype(jnp.bfloat16)
    whole_hidden = lax.all_to_all(partial_hidden, "tp", split_axis=0, concat_axis=1, tiled=True)
    shared_out = jnp.dot(whole_hidden, shared_down, preferred_element_type=jnp.float32)
    safe_target = jnp.where(kept_pair, destination_position, 0)
    picked = jnp.take(returned_rows, safe_target.reshape(-1), axis=0).reshape(
        local_rows, TOP, model_width
    )
    kept_weights = jnp.where(kept_pair, gates, jnp.float32(0.0))
    routed = jnp.sum(picked.astype(jnp.float32) * kept_weights[:, :, None], axis=1)
    return (values + shared_out + routed).astype(jnp.bfloat16)


def solution(mesh):
    placed = (
        P(("ep", "tp"), None),
        P(),
        P(("ep", "tp"), None),
        P(("ep", "tp"), None),
        P(("ep", "tp"), None),
        P(("ep", "tp"), None),
        P("ep", None, "tp"),
        P("ep", None, "tp"),
        P("ep", None, "tp"),
        P(None, "tp"),
        P(None, "tp"),
        P(),
    )
    return jax.shard_map(
        on_device, mesh=mesh, in_specs=placed, out_specs=P(("ep", "tp"), None), check_vma=False
    )
```

profile of v0, /device:TPU:0, one launch (start us, length us, event | category | flops | bytes accessed | tf_op | source)
XLA Modules:
  0.0 298.9 jit_solution(15551164740821854965)
XLA Ops:
  6.5 0.0 copy-start
  6.5 0.0 copy-start.1
  6.5 0.0 copy-start.3
  6.5 0.0 copy-start.6
  6.5 0.0 copy-start.7
  6.6 0.0 all-gather.9.cloned.1.call-start
  6.6 0.7 all-gather.9.cloned.1.call-update
  7.3 0.0 all-gather.11.cloned.1.call-start
  7.3 0.7 all-gather.11.cloned.1.call-update
  8.0 0.0 all-gather.7.cloned.1.call-start
  8.1 0.7 all-gather.7.cloned.1.call-update
  8.8 0.0 copy-done.1
  8.8 0.2 fusion.29
  9.0 0.0 copy-done.3
  9.0 0.2 fusion.31
  9.2 0.0 copy-start.2
  9.2 0.0 copy-done.6
  9.2 0.0 copy-done.5
  9.2 0.0 copy-done.7
  9.3 0.6 fusion.15
  9.9 1.3 convolution_convert_fusion
  11.2 100.4 %all_to_all.29 = bf16[8,2,64,2048]{3,2,1,0:T(8,128)(2,1)} all-to-all(bf16[8,2,64,2048]{3,2,1,0:T(8,128)(2,1)S(1)} %bitcast.62), channel_id=1, replica_groups=mesh['ep'=8,'tp'=4] {'ep'}, dimensions={0} | all-to-all | bytes 8388608 | tf_op jit(solution)/shard_map/all_to_all | solution.py:49
  111.5 0.0 copy-done.2
  111.5 9.2 %fusion.2 = f32[2,8,64,704]{3,2,1,0:T(8,128)} fusion(bf16[2,2048,704]{1,2,0:T(8,128)(2,1)} %all-gather.9.cloned.1.call-done, bf16[8,2,64,2048]{3,2,1,0:T(8,128)(2,1)} %all_to_all.29), kind=kOutput, calls=%fused_computation.4 | convolution fusion | flops 2952790016 | bytes 12845056 | tf_op jit(solution)/shard_map/iecd,edf->iecf/dot_general | solution.py:54
  120.7 24.3 %all-gather.7.cloned.1.call-done = bf16[2,2048,704]{1,2,0:T(8,128)(2,1)} async-done(((bf16[2,2048,176]{1,2,0:T(8,128)(2,1)}), bf16[2,2048,704]{1,2,0:T(8,128)(2,1)}) %all-gather.7.cloned.1.call-update) | async-done | bytes 5767184 | tf_op jit(solution)/shard_map/all_gather | solution.py:50
  145.0 13.1 %convert_bitcast_fusion = bf16[8,2,64,2048]{3,2,0,1:T(8,128)(2,1)} fusion(bf16[2,2048,704]{1,2,0:T(8,128)(2,1)} %all-gather.11.cloned.1.call-done, f32[2,8,64,704]{3,2,1,0:T(8,128)} %fusion.2, bf16[2,2048,704]{1,2,0:T(8,128)(2,1)} %all-gather.7.cloned.1.call-done, bf16[8,2,64,2048]{3,2,1,0:T(8,128)(2,1)} %all_to_all.29), kind=kOutput, calls=%fused_computation.8 | convolution fusion | flops 5912002560 | bytes 22806528 | tf_op jit(solution)/shard_map/iecf,edf->iecd/dot_general | solution.py:56
  158.1 4.7 %copy.39 = bf16[8,2,64,2048]{3,2,1,0:T(8,128)(2,1)} copy(bf16[8,2,64,2048]{3,2,0,1:T(8,128)(2,1)} %convert_bitcast_fusion) | data formatting | bytes 8388608 | tf_op jit(solution)/shard_map/convert_element_type | solution.py:58
  162.9 5.6 %all-to-all-start.2 = ((bf16[8,2,64,2048]{3,2,1,0:T(8,128)(2,1)}), bf16[8,2,64,2048]{3,2,1,0:T(8,128)(2,1)}, u32[]{:S(2)}, u32[]{:S(2)}) async-start(bf16[8,2,64,2048]{3,2,1,0:T(8,128)(2,1)} %copy.39), calls=%async_computation.2 | async-start | bytes 8388608 | tf_op jit(solution)/shard_map/all_to_all | solution.py:59
  168.5 0.0 all-gather.5.cloned.1.call-start
  168.6 0.5 all-gather.5.cloned.1.call-update
  169.1 0.1 copy.40
  169.2 0.1 reshape.66
  169.4 0.0 copy-done.4
  169.4 0.1 copy.41
  169.5 0.1 copy.36
  169.7 24.0 %all-gather.5.cloned.1.call-done = bf16[512,2048]{1,0:T(8,128)(2,1)} async-done(((bf16[128,2048]{1,0:T(8,128)(2,1)}), bf16[512,2048]{1,0:T(8,128)(2,1)}) %all-gather.5.cloned.1.call-update) | async-done | bytes 2097168 | tf_op jit(solution)/shard_map/all_gather | solution.py:61
  193.7 0.0 copy-done
  193.7 2.7 fusion.34
  196.4 0.0 copy-done.8
  196.4 2.4 fusion.28
  198.8 0.8 copy.55
  199.6 62.6 %all-to-all-done.2 = bf16[8,2,64,2048]{3,2,1,0:T(8,128)(2,1)} async-done(((bf16[8,2,64,2048]{3,2,1,0:T(8,128)(2,1)}), bf16[8,2,64,2048]{3,2,1,0:T(8,128)(2,1)}, u32[]{:S(2)}, u32[]{:S(2)}) %all-to-all-start.2) | async-done | bytes 4194336 | tf_op jit(solution)/shard_map/all_to_all | solution.py:59
  262.2 3.6 %all-to-all-start = ((bf16[4,128,352]{1,2,0:T(8,128)(2,1)}), bf16[4,128,352]{1,2,0:T(8,128)(2,1)S(1)}, u32[]{:S(2)}, u32[]{:S(2)}) async-start(bf16[4,128,352]{1,2,0:T(8,128)(2,1)} %bitcast.61), calls=%async_computation | async-start | bytes 720896 | tf_op jit(solution)/shard_map/all_to_all | solution.py:65
  265.9 9.9 %gather_fusion = bf16[768,2048]{1,0:T(8,128)(2,1)} fusion(bf16[1024,2048]{1,0:T(8,128)(2,1)} %bitcast.12, s32[1024]{0:T(1024)S(1)} %pad_clamp_fusion), kind=kCustom, calls=%fused_computation | custom fusion | bytes 6294528 | tf_op jit(solution)/shard_map/jit(_take)/gather | solution.py:68
  275.7 6.2 %gather.7 = bf16[128,6,2048]{2,1,0:T(8,128)(2,1)} reshape(bf16[768,2048]{1,0:T(8,128)(2,1)} %gather_fusion) | data formatting | bytes 6291456 | tf_op jit(solution)/shard_map/jit(_take)/gather | solution.py:68
  282.0 6.0 %multiply_reduce_fusion = f32[128,2048]{1,0:T(8,128)S(1)} fusion(f32[128,6]{1,0:T(8,128)S(1)} %copy.41, bf16[128,6,2048]{2,1,0:T(8,128)(2,1)} %gather.7, pred[128,6]{1,0:T(8,128)(4,1)S(1)} %copy.36), kind=kLoop, calls=%fused_computation.1 | loop fusion | flops 6029312 | bytes 4198144 | tf_op jit(solution)/shard_map/reduce_sum | solution.py:72
  287.9 0.0 all-to-all-done
  287.9 4.4 %fusion.17 = bf16[128,2048]{1,0:T(8,128)(2,1)} fusion(f32[128,2048]{1,0:T(8,128)S(1)} %multiply_reduce_fusion, bf16[128,1408]{0,1:T(8,128)(2,1)S(1)} %bitcast.63, bf16[1408,2048]{1,0:T(8,128)(2,1)} %param.23, bf16[128,2048]{1,0:T(8,128)(2,1)S(1)} %copy-done.1), kind=kOutput, calls=%fused_computation.24 | convolution fusion | flops 739246080 | bytes 8224768 | tf_op jit(solution)/shard_map/dot_general | solution.py:66
  (10 shorter events, 0.1 us)
Async XLA Ops:
  6.5 187.1 %copy-start = (bf16[2048,352]{0,1:T(8,128)(2,1)S(1)}, bf16[2048,352]{0,1:T(8,128)(2,1)}, u32[]{:S(2)}) copy-start(bf16[2048,352]{0,1:T(8,128)(2,1)} %param.21) | copy-start | bytes 4325380
  6.5 2.2 copy-start.1
  6.5 2.4 copy-start.3
  6.5 2.7 copy-start.6
  6.5 2.7 copy-start.5
  6.5 2.7 copy-start.7
  6.6 105.0 %all-gather.9.cloned.1.call-start = ((), (), s32[]{:S(2)}) async-start(), calls=%async_computation.5 | async-start | bytes 7208960 | tf_op jit(solution)/shard_map/all_gather | solution.py:51
  7.3 113.4 %all-gather.11.cloned.1.call-start = ((), (), s32[]{:S(2)}) async-start(), calls=%async_computation.6 | async-start | bytes 7208960 | tf_op jit(solution)/shard_map/all_gather | solution.py:52
  8.0 137.0 %all-gather.7.cloned.1.call-start = ((), (), s32[]{:S(2)}) async-start(), calls=%async_computation.4 | async-start | bytes 7208960 | tf_op jit(solution)/shard_map/all_gather | solution.py:50
  9.2 102.4 %copy-start.2 = (bf16[128,2048]{1,0:T(8,128)(2,1)}, bf16[128,2048]{1,0:T(8,128)(2,1)S(1)}, u32[]{:S(2)}) copy-start(bf16[128,2048]{1,0:T(8,128)(2,1)S(1)} %fusion.31) | copy-start | bytes 1572868
  162.9 6.5 %copy-start.4 = (f32[128,6]{0,1:T(8,128)S(1)}, f32[128,6]{0,1:T(8,128)}, u32[]{:S(2)}) copy-start(f32[128,6]{0,1:T(8,128)} %param.17) | copy-start | bytes 9220
  162.9 99.3 %all-to-all-start.2 = ((bf16[8,2,64,2048]{3,2,1,0:T(8,128)(2,1)}), bf16[8,2,64,2048]{3,2,1,0:T(8,128)(2,1)}, u32[]{:S(2)}, u32[]{:S(2)}) async-start(bf16[8,2,64,2048]{3,2,1,0:T(8,128)(2,1)} %copy.39), calls=%async_computation.2 | async-start | bytes 8388608 | tf_op jit(solution)/shard_map/all_to_all | solution.py:59
  168.5 25.1 %all-gather.5.cloned.1.call-start = ((), (), s32[]{:S(2)}) async-start(), calls=%async_computation.3 | async-start | bytes 2621440 | tf_op jit(solution)/shard_map/all_gather | solution.py:61
  193.7 2.7 copy-start.8
  262.2 25.7 %all-to-all-start = ((bf16[4,128,352]{1,2,0:T(8,128)(2,1)}), bf16[4,128,352]{1,2,0:T(8,128)(2,1)S(1)}, u32[]{:S(2)}, u32[]{:S(2)}) async-start(bf16[4,128,352]{1,2,0:T(8,128)(2,1)} %bitcast.61), calls=%async_computation | async-start | bytes 720896 | tf_op jit(solution)/shard_map/all_to_all | solution.py:65
Sparse Core Ops, SparseCore 0:
  8.9 46.0 all-gather.8
  56.6 43.3 all-gather.10
  101.6 43.3 all-gather.6
  170.6 23.0 all-gather.4
where the time goes:
time: 300 us; the launch traced here: 299 us
  waiting for transfers between devices  114 us (38%)
  blocking collectives  100 us (33%)
  matrix products  33.2 us (11%)
  local copies, waits for them, and re-layouts  22.2 us (7%)
  between operations  13.3 us (4%)
  starting transfers between devices  9.44 us (3%)
  other arithmetic  6.97 us (2%)
    all_to_all x1, blocking collectives, on_device(): lax.all_to_all(boxes, 'ep', split_axis=0, concat_axis=0, tiled=True)  100 us
    all_to_all x1, waiting for transfers between devices, on_device(): lax.all_to_all(expert_out, 'ep', split_axis=0, concat_axis=0, tiled=True)  62.6 us
    all_gather x1, waiting for transfers between devices, on_device(): gate_all = lax.all_gather(w_gate, 'tp', axis=2, tiled=True)  24.3 us
    all_gather x1, waiting for transfers between devices, on_device(): shard_piece = lax.all_gather(normed, 'tp', axis=0, tiled=True)  24 us
    gather x2, local copies, waits for them, and re-layouts, on_device(): jnp.take(returned_rows, safe_target.reshape(-1), axis=0)  16.1 us
    dot_general x1, matrix products, on_device(): jnp.einsum('iecf,edf->iecd', hidden, down_all, preferred_element_type=jnp...  13.1 us
    dot_general x1, matrix products, on_device(): jnp.einsum('iecd,edf->iecf', received, up_all, preferred_element_type=jnp...  9.17 us
  transfers between devices with their start and end apart: 6, of which 3 were waited for; matrix products, arithmetic and copies ran while one was open for 13% of the time, Pallas kernels for 0%

commit v1 on v0

--- a/solution.py
+++ b/solution.py
@@ -2,11 +2,45 @@
 import jax.numpy as jnp
 from jax import lax
 from jax.sharding import PartitionSpec as P
+from jax.lax import axis_index, axis_size, ppermute
 
 TOP = 6
 EXP_DEV = 2
 TOK_DEV = 128
 norm_eps = 1e-06
+
+
+def strings_get(raw, comm_axis, buf):
+    plain = axis_size(comm_axis)
+    arr_now = axis_index(comm_axis)
+    tall, block_out, local_out = (plain, arr_now, raw.shape[2])
+    stack_in = [(s, (s + 1) % tall) for s in range(tall)]
+    arrivals = [(q, no) for no, q in stack_in]
+    carry_out = ppermute(raw, comm_axis, stack_in)
+    u1 = ppermute(raw, comm_axis, arrivals)
+    g_now, res = (carry_out, u1)
+    big = buf(raw, block_out * local_out)
+    upper = big.shape[3]
+    b_next = jnp.zeros((*big.shape[:3], tall * upper, *big.shape[4:]), big.dtype)
+
+    def _map_quarters(b_next, big, near):
+        a_next = lax.dynamic_update_slice_in_dim(b_next, big, near * upper, axis=3)
+        return a_next
+
+    b_next = _map_quarters(b_next, big, block_out)
+    for rr in range(1, tall // 2 + 1):
+        base_arr, y2 = ((block_out - rr) % tall, (block_out + rr) % tall)
+        vec_out = (g_now, res)
+        if rr < tall // 2:
+            w_next = ppermute(g_now, comm_axis, stack_in)
+            long_array = ppermute(res, comm_axis, arrivals)
+            g_now, res = (w_next, long_array)
+        block_last = buf(vec_out[0], base_arr * local_out)
+        b_next = _map_quarters(b_next, block_last, base_arr)
+        if 2 * rr < tall:
+            piece_next = buf(vec_out[1], y2 * local_out)
+            b_next = _map_quarters(b_next, piece_next, y2)
+    return b_next
 
 
 def swiglu(left, right):
@@ -47,10 +81,15 @@
     ).astype(jnp.bfloat16)
     boxes = outgoing.reshape(n_expert_groups, EXP_DEV, capacity, model_width)
     received = lax.all_to_all(boxes, "ep", split_axis=0, concat_axis=0, tiled=True)
-    gate_all = lax.all_gather(w_gate, "tp", axis=2, tiled=True)
     up_all = lax.all_gather(w_up, "tp", axis=2, tiled=True)
     down_all = lax.all_gather(w_down, "tp", axis=2, tiled=True)
-    gate_act = jnp.einsum("iecd,edf->iecf", received, gate_all, preferred_element_type=jnp.float32)
+    gate_act = strings_get(
+        w_gate,
+        "tp",
+        buf=lambda own_block, offset: jnp.einsum(
+            "iecd,edf->iecf", received, own_block, preferred_element_type=jnp.float32
+        ),
+    )
     up_act = jnp.einsum("iecd,edf->iecf", received, up_all, preferred_element_type=jnp.float32)
     hidden = swiglu(gate_act, up_act).astype(jnp.bfloat16)
     expert_out = jnp.einsum(

time: 300 us -> 312 us (1.040)
  blocking collectives: 100 us -> 0 us
  waiting for transfers between devices: 114 us -> 178 us
  local copies, waits for them, and re-layouts: 22.2 us -> 51.2 us
  matrix products: 33.2 us -> 41.5 us
  starting transfers between devices: 9.44 us -> 17.6 us
    all_to_all x1 -> x0, blocking collectives: 100 us -> none  [on_device(): lax.all_to_all(boxes, 'ep', split_axis=0, concat_axis=0, tiled=True)]
    ppermute x0 -> x3, waiting for transfers between devices: none -> 59.6 us  [the longest x1 59.6 us: strings_get(): carry_out = ppermute(raw, comm_axis, stack_in)]
    all_to_all x0 -> x1, waiting for transfers between devices: none -> 31.1 us  [on_device(): lax.all_to_all(boxes, 'ep', split_axis=0, concat_axis=0, tiled=True)]
    dynamic_update_slice x0 -> x4, local copies, waits for them, and re-layouts: none -> 27 us  [_map_quarters(): a_next = lax.dynamic_update_slice_in_dim(b_next, big, near * upper, axis=3)]
    all_gather x1 -> x0, waiting for transfers between devices: 24.3 us -> none  [on_device(): gate_all = lax.all_gather(w_gate, 'tp', axis=2, tiled=True)]
    all_to_all x0 -> x1, starting transfers between devices: none -> 7.31 us  [on_device(): lax.all_to_all(boxes, 'ep', split_axis=0, concat_axis=0, tiled=True)]
    dot_general x1 -> x4, matrix products: 9.17 us -> 15.6 us  [on_device(): jnp.einsum('iecd,edf->iecf', received, own_block, preferred_element_type=...]
  transfers between devices with their start and end apart: 6 -> 9, of which waited for: 3 -> 4; matrix products, arithmetic and copies ran while one was open for 13% -> 26% of each run, Pallas kernels for 0% -> 0%
where the time goes in v1:
time: 312 us; the launch traced here: 311 us
  waiting for transfers between devices  178 us (57%)
  local copies, waits for them, and re-layouts  51.2 us (16%)
  matrix products  41.5 us (13%)
  starting transfers between devices  17.6 us (6%)
  between operations  13.3 us (4%)
  other arithmetic  9.82 us (3%)
    all_to_all x1, waiting for transfers between devices, on_device(): lax.all_to_all(expert_out, 'ep', split_axis=0, concat_axis=0, tiled=True)  60.3 us
    ppermute x1, waiting for transfers between devices, strings_get(): carry_out = ppermute(raw, comm_axis, stack_in)  59.6 us
    all_to_all x1, waiting for transfers between devices, on_device(): lax.all_to_all(boxes, 'ep', split_axis=0, concat_axis=0, tiled=True)  31.1 us
    dynamic_update_slice x4, local copies, waits for them, and re-layouts, _map_quarters(): a_next = lax.dynamic_update_slice_in_dim(b_next, big, near * upper, axis=3)  27 us
    all_gather x1, waiting for transfers between devices, on_device(): shard_piece = lax.all_gather(normed, 'tp', axis=0, tiled=True)  25 us
    gather x2, local copies, waits for them, and re-layouts, on_device(): jnp.take(returned_rows, safe_target.reshape(-1), axis=0)  16.1 us
    dot_general x4, matrix products, on_device(): jnp.einsum('iecd,edf->iecf', received, own_block, preferred_element_type=...  15.6 us
    dot_general x1, matrix products, on_device(): jnp.einsum('iecf,edf->iecd', hidden, down_all, preferred_element_type=jnp...  13.1 us
  transfers between devices with their start and end apart: 9, of which 4 were waited for; matrix products, arithmetic and copies ran while one was open for 26% of the time, Pallas kernels for 0%

profile of v1, /device:TPU:0, one launch (start us, length us, event | category | flops | bytes accessed | tf_op | source)
XLA Modules:
  0.0 311.2 jit_solution(2098325018047507510)
XLA Ops:
  6.5 0.0 all-gather.6.cloned.1.call-start
  6.5 0.7 all-gather.6.cloned.1.call-update
  7.3 1.2 fusion.55
  8.5 0.7 compare_and_fusion
  9.2 0.6 fusion.8
  9.8 1.2 fusion.57
  11.1 0.0 copy-start.2
  11.1 3.2 %convolution_convert_fusion = bf16[1024,2048]{1,0:T(8,128)(2,1)} fusion(pred[128,1024]{1,0:T(8,128)(4,1)S(1)} %fusion.8, bf16[128,2048]{1,0:T(8,128)(2,1)S(1)} %fusion.57), kind=kOutput, calls=%fused_computation.7 | convolution fusion | flops 538968064 | bytes 4849664 | tf_op jit(solution)/shard_map/dot_general | solution.py:79
  14.3 7.3 %all-to-all-start.1 = ((bf16[8,2,64,2048]{3,2,1,0:T(8,128)(2,1)}), bf16[8,2,64,2048]{3,2,1,0:T(8,128)(2,1)}, u32[]{:S(2)}, u32[]{:S(2)}) async-start(bf16[8,2,64,2048]{3,2,1,0:T(8,128)(2,1)} %bitcast.78), calls=%async_computation.1 | async-start | bytes 8388608 | tf_op jit(solution)/shard_map/all_to_all | solution.py:83
  21.6 0.0 all-gather.8.cloned.1.call-start
  21.7 0.7 all-gather.8.cloned.1.call-update
  22.4 0.1 collective-permute-start
  22.5 1.7 collective-permute-start.1
  24.2 59.6 %collective-permute-done = bf16[2,2048,176]{1,2,0:T(8,128)(2,1)} collective-permute-done((bf16[2,2048,176]{1,2,0:T(8,128)(2,1)}, bf16[2,2048,176]{1,2,0:T(8,128)(2,1)}, u32[]{:S(2)}, u32[]{:S(2)}) %collective-permute-start) | collective-permute-done | bytes 1441824 | tf_op jit(solution)/shard_map/ppermute | solution.py:19
  83.8 0.0 collective-permute-start.2
  83.8 31.1 %all-to-all-done.1 = bf16[8,2,64,2048]{3,2,1,0:T(8,128)(2,1)} async-done(((bf16[8,2,64,2048]{3,2,1,0:T(8,128)(2,1)}), bf16[8,2,64,2048]{3,2,1,0:T(8,128)(2,1)}, u32[]{:S(2)}, u32[]{:S(2)}) %all-to-all-start.1) | async-done | bytes 4194336 | tf_op jit(solution)/shard_map/all_to_all | solution.py:83
  114.9 3.9 %fusion.33 = f32[8,2,64,176]{3,2,0,1:T(8,128)S(1)} fusion(bf16[2,2048,176]{1,2,0:T(8,128)(2,1)} %param.18, bf16[8,2,64,2048]{3,2,1,0:T(8,128)(2,1)} %all-to-all-done.1), kind=kOutput, calls=%fused_computation.32 | convolution fusion | flops 738197504 | bytes 6356992 | tf_op jit(solution)/shard_map/iecd,edf->iecf/dot_general | solution.py:89
  118.8 2.0 broadcast_in_dim.26
  120.8 5.8 %dynamic_update_slice.12 = f32[8,2,64,704]{3,2,0,1:T(8,128)} dynamic-update-slice(f32[8,2,64,704]{3,2,0,1:T(8,128)} %broadcast_in_dim.26, f32[8,2,64,176]{3,2,0,1:T(8,128)S(1)} %fusion.33, s32[]{:T(128)} %constant.56.clone.1, s32[]{:T(128)} %constant.56.clone.1, s32[]{:T(128)} %constant.56.clone.1, s32[]{:T(128)S(6)} %select_n.59) | dynamic-update-slice | bytes 1441796 | tf_op jit(solution)/shard_map/dynamic_update_slice | solution.py:27
  126.7 3.9 %fusion.38 = f32[8,2,64,176]{3,2,0,1:T(8,128)S(1)} fusion(bf16[2,2048,176]{1,2,0:T(8,128)(2,1)} %collective-permute-done, bf16[8,2,64,2048]{3,2,1,0:T(8,128)(2,1)} %all-to-all-done.1), kind=kOutput, calls=%fused_computation.33 | convolution fusion | flops 738197504 | bytes 6356992 | tf_op jit(solution)/shard_map/iecd,edf->iecf/dot_general | solution.py:89
  130.6 6.6 %dynamic_update_slice.13 = f32[8,2,64,704]{3,2,0,1:T(8,128)} dynamic-update-slice(f32[8,2,64,704]{3,2,0,1:T(8,128)} %dynamic_update_slice.12, f32[8,2,64,176]{3,2,0,1:T(8,128)S(1)} %fusion.38, s32[]{:T(128)} %constant.56.clone.1, s32[]{:T(128)} %constant.56.clone.1, s32[]{:T(128)} %constant.56.clone.1, s32[]{:T(128)S(6)} %select_n.61) | dynamic-update-slice | bytes 1441796 | tf_op jit(solution)/shard_map/dynamic_update_slice | solution.py:27
  137.2 0.0 collective-permute-done.1
  137.2 3.9 %fusion.43 = f32[8,2,64,176]{3,2,0,1:T(8,128)S(1)} fusion(bf16[2,2048,176]{1,2,0:T(8,128)(2,1)} %collective-permute-done.1, bf16[8,2,64,2048]{3,2,1,0:T(8,128)(2,1)} %all-to-all-done.1), kind=kOutput, calls=%fused_computation.34 | convolution fusion | flops 738197504 | bytes 6356992 | tf_op jit(solution)/shard_map/iecd,edf->iecf/dot_general | solution.py:89
  141.1 7.3 %dynamic_update_slice.14 = f32[8,2,64,704]{3,2,0,1:T(8,128)} dynamic-update-slice(f32[8,2,64,704]{3,2,0,1:T(8,128)} %dynamic_update_slice.13, f32[8,2,64,176]{3,2,0,1:T(8,128)S(1)} %fusion.43, s32[]{:T(128)} %constant.56.clone.1, s32[]{:T(128)} %constant.56.clone.1, s32[]{:T(128)} %constant.56.clone.1, s32[]{:T(128)S(6)} %select_n.63) | dynamic-update-slice | bytes 1441796 | tf_op jit(solution)/shard_map/dynamic_update_slice | solution.py:27
  148.4 0.0 collective-permute-done.2
  148.4 3.9 %fusion.48 = f32[8,2,64,176]{3,2,0,1:T(8,128)S(1)} fusion(bf16[2,2048,176]{1,2,0:T(8,128)(2,1)} %collective-permute-done.2, bf16[8,2,64,2048]{3,2,1,0:T(8,128)(2,1)} %all-to-all-done.1), kind=kOutput, calls=%fused_computation.35 | convolution fusion | flops 738197504 | bytes 6356992 | tf_op jit(solution)/shard_map/iecd,edf->iecf/dot_general | solution.py:89
  152.3 7.3 %dynamic_update_slice.15 = f32[8,2,64,704]{3,2,0,1:T(8,128)} dynamic-update-slice(f32[8,2,64,704]{3,2,0,1:T(8,128)} %dynamic_update_slice.14, f32[8,2,64,176]{3,2,0,1:T(8,128)S(1)} %fusion.48, s32[]{:T(128)} %constant.56.clone.1, s32[]{:T(128)} %constant.56.clone.1, s32[]{:T(128)} %constant.56.clone.1, s32[]{:T(128)S(6)} %select_n.65) | dynamic-update-slice | bytes 1441796 | tf_op jit(solution)/shard_map/dynamic_update_slice | solution.py:27
  159.6 13.1 %convert_bitcast_fusion = bf16[8,2,64,2048]{3,2,0,1:T(8,128)(2,1)} fusion(bf16[2,2048,704]{1,2,0:T(8,128)(2,1)} %all-gather.8.cloned.1.call-done, f32[8,2,64,704]{3,2,0,1:T(8,128)} %dynamic_update_slice.15, bf16[2,2048,704]{1,2,0:T(8,128)(2,1)} %all-gather.6.cloned.1.call-done, bf16[8,2,64,2048]{3,2,1,0:T(8,128)(2,1)} %all-to-all-done.1), kind=kOutput, calls=%fused_computation.6 | convolution fusion | flops 5912002560 | bytes 22806528 | tf_op jit(solution)/shard_map/iecf,edf->iecd/dot_general | solution.py:95
  172.7 4.7 %copy.45 = bf16[8,2,64,2048]{3,2,1,0:T(8,128)(2,1)} copy(bf16[8,2,64,2048]{3,2,0,1:T(8,128)(2,1)} %convert_bitcast_fusion) | data formatting | bytes 8388608 | tf_op jit(solution)/shard_map/convert_element_type | solution.py:97
  177.4 4.7 %all-to-all-start.2 = ((bf16[8,2,64,2048]{3,2,1,0:T(8,128)(2,1)}), bf16[8,2,64,2048]{3,2,1,0:T(8,128)(2,1)}, u32[]{:S(2)}, u32[]{:S(2)}) async-start(bf16[8,2,64,2048]{3,2,1,0:T(8,128)(2,1)} %copy.45), calls=%async_computation.2 | async-start | bytes 8388608 | tf_op jit(solution)/shard_map/all_to_all | solution.py:98
  182.1 0.3 all-gather.4.cloned.1.call-start
  182.4 0.5 all-gather.4.cloned.1.call-update
  182.8 0.1 copy.46
  182.9 0.1 reshape.66
  183.1 0.1 copy.47
  183.2 0.1 copy.39
  183.4 25.0 %all-gather.4.cloned.1.call-done = bf16[512,2048]{1,0:T(8,128)(2,1)} async-done(((bf16[128,2048]{1,0:T(8,128)(2,1)}), bf16[512,2048]{1,0:T(8,128)(2,1)}) %all-gather.4.cloned.1.call-update) | async-done | bytes 2097168 | tf_op jit(solution)/shard_map/all_gather | solution.py:100
  208.4 2.7 fusion.60
  211.1 0.0 copy-done.4
  211.1 2.4 fusion.54
  213.6 0.8 copy.78
  214.4 60.3 %all-to-all-done.2 = bf16[8,2,64,2048]{3,2,1,0:T(8,128)(2,1)} async-done(((bf16[8,2,64,2048]{3,2,1,0:T(8,128)(2,1)}), bf16[8,2,64,2048]{3,2,1,0:T(8,128)(2,1)}, u32[]{:S(2)}, u32[]{:S(2)}) %all-to-all-start.2) | async-done | bytes 4194336 | tf_op jit(solution)/shard_map/all_to_all | solution.py:98
  274.6 3.5 %all-to-all-start = ((bf16[4,128,352]{1,2,0:T(8,128)(2,1)}), bf16[4,128,352]{1,2,0:T(8,128)(2,1)S(1)}, u32[]{:S(2)}, u32[]{:S(2)}) async-start(bf16[4,128,352]{1,2,0:T(8,128)(2,1)} %bitcast.77), calls=%async_computation | async-start | bytes 720896 | tf_op jit(solution)/shard_map/all_to_all | solution.py:104
  278.1 9.8 %gather_fusion = bf16[768,2048]{1,0:T(8,128)(2,1)} fusion(bf16[1024,2048]{1,0:T(8,128)(2,1)} %bitcast.21, s32[1024]{0:T(1024)S(1)} %pad_clamp_fusion), kind=kCustom, calls=%fused_computation | custom fusion | bytes 6294528 | tf_op jit(solution)/shard_map/jit(_take)/gather | solution.py:107
  287.9 6.2 %gather.7 = bf16[128,6,2048]{2,1,0:T(8,128)(2,1)} reshape(bf16[768,2048]{1,0:T(8,128)(2,1)} %gather_fusion) | data formatting | bytes 6291456 | tf_op jit(solution)/shard_map/jit(_take)/gather | solution.py:107
  294.2 6.0 %multiply_reduce_fusion = f32[128,2048]{1,0:T(8,128)S(1)} fusion(f32[128,6]{1,0:T(8,128)S(1)} %copy.47, bf16[128,6,2048]{2,1,0:T(8,128)(2,1)} %gather.7, pred[128,6]{1,0:T(8,128)(4,1)S(1)} %copy.39), kind=kLoop, calls=%fused_computation.1 | loop fusion | flops 6029312 | bytes 4198144 | tf_op jit(solution)/shard_map/reduce_sum | solution.py:111
  300.2 0.0 all-to-all-done
  300.2 4.4 %fusion.10 = bf16[128,2048]{1,0:T(8,128)(2,1)} fusion(f32[128,2048]{1,0:T(8,128)S(1)} %multiply_reduce_fusion, bf16[128,1408]{0,1:T(8,128)(2,1)S(1)} %bitcast.79, bf16[1408,2048]{1,0:T(8,128)(2,1)} %param.23, bf16[128,2048]{1,0:T(8,128)(2,1)S(1)} %copy-done.1), kind=kOutput, calls=%fused_computation.15 | convolution fusion | flops 739246080 | bytes 8224768 | tf_op jit(solution)/shard_map/dot_general | solution.py:105
  (14 shorter events, 0.1 us)
Async XLA Ops:
  6.5 201.9 %copy-start = (bf16[2048,352]{0,1:T(8,128)(2,1)S(1)}, bf16[2048,352]{0,1:T(8,128)(2,1)}, u32[]{:S(2)}) copy-start(bf16[2048,352]{0,1:T(8,128)(2,1)} %param.21) | copy-start | bytes 4325380
  6.5 153.0 %all-gather.6.cloned.1.call-start = ((), (), s32[]{:S(2)}) async-start(), calls=%async_computation.4 | async-start | bytes 7208960 | tf_op jit(solution)/shard_map/all_gather | solution.py:84
  11.1 3.3 %copy-start.2 = (bf16[128,2048]{1,0:T(8,128)(2,1)}, bf16[128,2048]{1,0:T(8,128)(2,1)S(1)}, u32[]{:S(2)}) copy-start(bf16[128,2048]{1,0:T(8,128)(2,1)S(1)} %fusion.57) | copy-start | bytes 1572868
  14.3 100.6 %all-to-all-start.1 = ((bf16[8,2,64,2048]{3,2,1,0:T(8,128)(2,1)}), bf16[8,2,64,2048]{3,2,1,0:T(8,128)(2,1)}, u32[]{:S(2)}, u32[]{:S(2)}) async-start(bf16[8,2,64,2048]{3,2,1,0:T(8,128)(2,1)} %bitcast.78), calls=%async_computation.1 | async-start | bytes 8388608 | tf_op jit(solution)/shard_map/all_to_all | solution.py:83
  21.6 137.9 %all-gather.8.cloned.1.call-start = ((), (), s32[]{:S(2)}) async-start(), calls=%async_computation.5 | async-start | bytes 7208960 | tf_op jit(solution)/shard_map/all_gather | solution.py:85
  22.4 61.4 %collective-permute-start = (bf16[2,2048,176]{1,2,0:T(8,128)(2,1)}, bf16[2,2048,176]{1,2,0:T(8,128)(2,1)}, u32[]{:S(2)}, u32[]{:S(2)}) collective-permute-start(bf16[2,2048,176]{1,2,0:T(8,128)(2,1)} %param.18), channel_id=1, source_target_pairs={{0,1},{1,2},{2,3},{3,0},{4,5},{5,6},{6,7},{7,4},{8,9},{9,10},{10,1... | collective-permute-start | bytes 4325384 | tf_op jit(solution)/shard_map/ppermute | solution.py:19
  22.5 114.7 %collective-permute-start.1 = (bf16[2,2048,176]{1,2,0:T(8,128)(2,1)}, bf16[2,2048,176]{1,2,0:T(8,128)(2,1)}, u32[]{:S(2)}, u32[]{:S(2)}) collective-permute-start(bf16[2,2048,176]{1,2,0:T(8,128)(2,1)} %param.18), channel_id=1, source_target_pairs={{1,0},{2,1},{3,2},{0,3},{5,4},{6,5},{7,6},{4,7},{9,8},{10,9},{11,1... | collective-permute-start | bytes 4325384 | tf_op jit(solution)/shard_map/ppermute | solution.py:20
  83.8 64.6 %collective-permute-start.2 = (bf16[2,2048,176]{1,2,0:T(8,128)(2,1)}, bf16[2,2048,176]{1,2,0:T(8,128)(2,1)}, u32[]{:S(2)}, u32[]{:S(2)}) collective-permute-start(bf16[2,2048,176]{1,2,0:T(8,128)(2,1)} %collective-permute-done), channel_id=1, source_target_pairs={{0,1},{1,2},{2,3},{3,0},{4,5},{5,6},{6,7},{7,4},{8,9},{9,10},{10,1... | collective-permute-start | bytes 4325384 | tf_op jit(solution)/shard_map/ppermute | solution.py:35
  177.4 5.7 %copy-start.3 = (f32[128,6]{0,1:T(8,128)S(1)}, f32[128,6]{0,1:T(8,128)}, u32[]{:S(2)}) copy-start(f32[128,6]{0,1:T(8,128)} %param.17) | copy-start | bytes 9220
  177.4 97.2 %all-to-all-start.2 = ((bf16[8,2,64,2048]{3,2,1,0:T(8,128)(2,1)}), bf16[8,2,64,2048]{3,2,1,0:T(8,128)(2,1)}, u32[]{:S(2)}, u32[]{:S(2)}) async-start(bf16[8,2,64,2048]{3,2,1,0:T(8,128)(2,1)} %copy.45), calls=%async_computation.2 | async-start | bytes 8388608 | tf_op jit(solution)/shard_map/all_to_all | solution.py:98
  182.1 26.3 %all-gather.4.cloned.1.call-start = ((), (), s32[]{:S(2)}) async-start(), calls=%async_computation.3 | async-start | bytes 2621440 | tf_op jit(solution)/shard_map/all_gather | solution.py:100
  208.4 2.7 copy-start.4
  274.6 25.5 %all-to-all-start = ((bf16[4,128,352]{1,2,0:T(8,128)(2,1)}), bf16[4,128,352]{1,2,0:T(8,128)(2,1)S(1)}, u32[]{:S(2)}, u32[]{:S(2)}) async-start(bf16[4,128,352]{1,2,0:T(8,128)(2,1)} %bitcast.77), calls=%async_computation | async-start | bytes 720896 | tf_op jit(solution)/shard_map/all_to_all | solution.py:104
  294.2 6.0 %copy-start.1 = (bf16[128,2048]{1,0:T(8,128)(2,1)S(1)}, bf16[128,2048]{1,0:T(8,128)(2,1)}, u32[]{:S(2)}) copy-start(bf16[128,2048]{1,0:T(8,128)(2,1)} %param.12) | copy-start | bytes 1572868
Sparse Core Ops, SparseCore 0:
  8.9 73.4 all-gather.5
  84.0 51.0 all-gather.7
  184.5 23.9 all-gather.3
